TPU v7x, 8 devices: a whole 2x2x1 slice. The times are simulated.
8 devices in a mesh: rep: 2 (over z, y), blk: 4 (over x, core).
Axes of the slice: x: 2, y: 2, z: 1, core: 2. Of those that a mesh axis runs over, the one named last changes fastest.
Arguments:
- ratings: float32 [4096, 16384], P(None, ('rep', 'blk')), parts along dimension 1
- observed: int32 [4096, 16384], P(None, ('rep', 'blk')), parts along dimension 1
- user_init: float32 [8192, 256], P(('rep', 'blk')), parts along dimension 0
- item_init: float32 [16384, 256], P(('rep', 'blk')), parts along dimension 0
- lr_scale: float32 [64, 1], replicated
Outputs:
- output 1: float32 [8192, 256], P(('rep', 'blk')), parts along dimension 0
- output 2: float32 [16384, 256], P(('rep', 'blk')), parts along dimension 0
There are 2 independent parts. A program takes and returns all parts, laid end to end along the dimension named above; an argument that names none is the same for every part.
All inputs are finite; a program needn't handle non-finite values.
Results may differ from a plain program's by a relative error of at most 0.001.
Values are sent between devices in bfloat16 or wider.
A program may use at most 1 GiB of HBM per device.

v0:
```python
import math
import jax
import jax.numpy as jnp
from jax import lax
from jax.sharding import PartitionSpec as P

LAMBDA = 0.05


def stratum_steps(users_cur, items_cur, rate_blk, mask_blk, lr_row, base_eta):
    def one_step(step_idx, step_state):
        users_now, items_now = step_state
        users_bf = users_now.astype(jnp.bfloat16)
        items_bf = items_now.astype(jnp.bfloat16)
        approx = jnp.einsum("ar,br->ab", users_bf, items_bf, preferred_element_type=jnp.float32)
        errors = jnp.where(mask_blk != 0, approx - rate_blk, 0.0).astype(jnp.bfloat16)
        grad_u = jnp.einsum("ab,br->ar", errors, items_bf, preferred_element_type=jnp.float32) + LAMBDA * users_now
        grad_v = jnp.einsum("ab,ar->br", errors, users_bf, preferred_element_type=jnp.float32) + LAMBDA * items_now
        step_size = base_eta * lr_row[step_idx]
        return users_now - step_size * grad_u, items_now - step_size * grad_v

    return lax.fori_loop(0, lr_row.shape[0], one_step, (users_cur, items_cur))


def solution(mesh):
    group_size = mesh.shape["blk"]
    send_perm = [(source, (source - 1) % group_size) for source in range(group_size)]

    def local_run(rate_loc, mask_loc, user_loc, item_loc, lr_scale):
        block_rows, rank_dim = user_loc.shape
        cols_dev = item_loc.shape[0]
        base_eta = math.sqrt(rank_dim) / (4.0 * (cols_dev + 2 * rank_dim))
        my_index = lax.axis_index("blk")

        def sub_epoch(t_index, loop_state):
            users_cur, items_cur = loop_state
            row_start = ((my_index + t_index) % group_size) * block_rows
            rate_blk = lax.dynamic_slice_in_dim(rate_loc, row_start, block_rows, 0)
            mask_blk = lax.dynamic_slice_in_dim(mask_loc, row_start, block_rows, 0)
            users_cur, items_cur = stratum_steps(users_cur, items_cur, rate_blk, mask_blk, lr_scale[t_index], base_eta)
            users_cur = lax.ppermute(users_cur, "blk", send_perm)
            return users_cur, items_cur

        return lax.fori_loop(0, lr_scale.shape[0], sub_epoch, (user_loc, item_loc))

    spec_cols = P(None, ("rep", "blk"))
    spec_rows = P(("rep", "blk"), None)
    mapped = jax.shard_map(local_run, mesh=mesh, in_specs=(spec_cols, spec_cols, spec_rows, spec_rows, P(None, None)), out_specs=(spec_rows, spec_rows), check_vma=False)
    return mapped
```

profile of v0, /device:TPU:1, one launch (start us, length us, event | category | flops | bytes accessed | tf_op | source)
XLA Modules:
  0.0 1679.0 jit_solution(10412569030737424035)
XLA Ops:
  2.6 1674.8 %while.29 = (s32[]{:T(128)}, f32[1024,256]{1,0:T(8,128)S(1)}, f32[2048,256]{1,0:T(8,128)S(1)}, f32[64,1]{0,1:T(1,128)S(1)}, s32[]{:T(128)}, /*index=5*/s32[4096,...) while((s32[]{:T(128)}, f32[1024,256]{1,0:T(8,128)S(1)}, ...), condition=%wide.region_1.2_spmd, body=%wide.region_0.1_spmd.sunk | while | flops 3234332672 | bytes 65012096 | solution.py:44
  18.2 10.2 collective-permute-done
  71.3 9.3 collective-permute-done
  97.5 9.3 collective-permute-done
  228.3 9.3 collective-permute-done
  254.4 9.3 collective-permute-done
  385.2 9.3 collective-permute-done
  411.3 9.3 collective-permute-done
  542.1 9.3 collective-permute-done
  568.3 9.3 collective-permute-done
  699.1 9.3 collective-permute-done
  725.2 9.3 collective-permute-done
  856.0 9.3 collective-permute-done
  882.2 9.3 collective-permute-done
  1012.9 9.3 collective-permute-done
  1039.1 9.3 collective-permute-done
  1169.9 9.3 collective-permute-done
  1196.0 9.3 collective-permute-done
  1326.8 9.3 collective-permute-done
  1353.0 9.3 collective-permute-done
  1483.7 9.3 collective-permute-done
  1509.9 9.3 collective-permute-done
  1640.7 9.3 collective-permute-done
  1666.8 9.3 collective-permute-done
  (563 shorter events, 1461.4 us)
Async XLA Ops:
  13.3 15.1 collective-permute-start
  40.3 14.2 collective-permute-start
  66.4 14.2 collective-permute-start
  118.7 14.2 collective-permute-start
  144.9 14.2 collective-permute-start
  197.2 14.2 collective-permute-start
  223.4 14.2 collective-permute-start
  249.5 14.2 collective-permute-start
  275.7 14.2 collective-permute-start
  380.3 14.2 collective-permute-start
  406.4 14.2 collective-permute-start
  432.6 14.2 collective-permute-start
  537.2 14.2 collective-permute-start
  563.4 14.2 collective-permute-start
  641.9 14.2 collective-permute-start
  720.3 14.2 collective-permute-start
  772.6 14.2 collective-permute-start
  798.8 14.2 collective-permute-start
  824.9 14.2 collective-permute-start
  929.6 14.2 collective-permute-start
  955.7 14.2 collective-permute-start
  981.9 14.2 collective-permute-start
  1060.3 14.2 collective-permute-start
  1086.5 14.2 collective-permute-start
  (109 other events, 767.1 us)
where the time goes:
time: 1690 us; the launch traced here: 1680 us
  matrix products  954 us (56%)
  waiting for transfers between devices  597 us (35%)
  local copies, waits for them, and re-layouts  82.2 us (5%)
  other arithmetic  42.6 us (3%)
    ppermute x64, waiting for transfers between devices, sub_epoch(): users_cur = lax.ppermute(users_cur, 'blk', send_perm)  597 us
    dot_general x64, matrix products, one_step(): jnp.einsum('ar,br->ab', users_bf, items_bf, preferred_element_type=jnp.fl...  452 us
    dot_general x64, matrix products, one_step(): jnp.einsum('ab,ar->br', errors, users_bf, preferred_element_type=jnp.floa...  313 us
    dot_general x64, matrix products, one_step(): jnp.einsum('ab,br->ar', errors, items_bf, preferred_element_type=jnp.floa...  189 us
    while x192, local copies, waits for them, and re-layouts  78.7 us
    mul x64, other arithmetic, one_step(): step_size = base_eta * lr_row[step_idx]  42.6 us
  transfers between devices with their start and end apart: 64, of which 64 were waited for; matrix products, arithmetic and copies ran while one was open for 19% of the time, Pallas kernels for 0%

commit v1 on v0

v1 whole, which is shorter than its diff:
```python
import functools
import math

import jax
import jax.numpy as jnp
from jax import lax
from jax.experimental import pallas as pl
from jax.experimental.pallas import tpu as pltpu
from jax.sharding import PartitionSpec as P

LAMBDA = 0.05
MESH = pl.DeviceIdType.MESH
CHUNK = 256
TILE = 512
STAGES = 3


def run_kernel(group, epochs_t, base_eta, lr_ref, r_hbm, m_hbm, u_hbm, v_hbm, uo_hbm, vo_hbm,
               rate, mask, v, vb, gv, err, inb, outb, load_sem, r_sem, m_sem, send_sem, recv_sem, home_sem, credit):
    rep, me = lax.axis_index("rep"), lax.axis_index("blk")
    left, right = lax.rem(me + group - 1, group), lax.rem(me + 1, group)
    chunks = inb.shape[1]
    items = v.shape[0]
    loads = group * chunks

    def row_block(g):
        return lax.rem(me + g // chunks, group) * chunks + lax.rem(g, chunks)

    def rate_load(g):
        where = row_block(g)
        return pltpu.make_async_copy(r_hbm.at[pl.ds(pl.multiple_of(where * CHUNK, CHUNK), CHUNK)], rate.at[where], r_sem.at[lax.rem(g, STAGES)])

    def mask_load(g):
        where = row_block(g)
        slot = lax.rem(g, STAGES)
        return pltpu.make_async_copy(m_hbm.at[pl.ds(pl.multiple_of(where * CHUNK, CHUNK), CHUNK)], mask.at[slot], m_sem.at[slot])

    def send(t, c):
        slot = lax.rem(t, 2)
        return pltpu.make_async_remote_copy(
            src_ref=outb.at[slot, c], dst_ref=inb.at[1 - slot, c], send_sem=send_sem.at[slot, c],
            recv_sem=recv_sem.at[1 - slot, c], device_id=(rep, left), device_id_type=MESH)

    def send_home(t, c):
        slot = lax.rem(t, 2)
        return pltpu.make_async_remote_copy(
            src_ref=outb.at[slot, c], dst_ref=uo_hbm.at[pl.ds(pl.multiple_of(c * CHUNK, CHUNK), CHUNK)], send_sem=send_sem.at[slot, c],
            recv_sem=home_sem.at[c], device_id=(rep, left), device_id_type=MESH)

    def user_load(c):
        return pltpu.make_async_copy(u_hbm.at[pl.ds(c * CHUNK, CHUNK)], inb.at[0, c], recv_sem.at[0, c])

    v_load = pltpu.make_async_copy(v_hbm, v, load_sem)
    v_load.start()
    user_load(0).start()
    rate_load(0).start()
    mask_load(0).start()
    for c in range(1, chunks):
        user_load(c).start()
    rate_load(1).start()
    mask_load(1).start()

    barrier = pltpu.get_barrier_semaphore()
    for neighbour in (left, right):
        pl.semaphore_signal(barrier, inc=1, device_id=(rep, neighbour), device_id_type=MESH)
    pl.semaphore_wait(barrier, 2)

    gv[...] = jnp.zeros_like(gv)
    v_load.wait()
    vb[...] = v[...].astype(jnp.bfloat16)

    def chunk_step(t, c, step_size, first):
        slot = lax.rem(t, 2)
        if first:
            g = t * chunks + c

            @pl.when(g + 2 < loads)
            def _():
                rate_load(g + 2).start()
                mask_load(g + 2).start()

            rate_load(g).wait()
            mask_load(g).wait()

        @pl.when(t == 0)
        def _():
            pltpu.make_async_copy(u_hbm.at[pl.ds(0, CHUNK)], inb.at[0, c], recv_sem.at[0, c]).wait()

        @pl.when(t > 0)
        def _():
            send(t - 1, c).wait_recv()

        @pl.when(t >= 2)
        def _():
            send(t, c).wait_send()

        where = lax.rem(me + t, group) * chunks + c
        users_bf = inb[slot, c].astype(jnp.bfloat16)
        for n in range(items // TILE):
            cols = pl.ds(n * TILE, TILE)
            approx = lax.dot_general(users_bf, vb[cols, :], (((1,), (1,)), ((), ())), preferred_element_type=jnp.float32)
            rates = rate[where, :, cols]
            if first:
                seen = mask[lax.rem(t * chunks + c, STAGES), :, cols] != 0
                rate[where, :, cols] = jnp.where(seen, rates, jnp.inf)
            else:
                seen = rates < jnp.inf
            err[:, cols] = jnp.where(seen, approx - rates, 0.0).astype(jnp.bfloat16)
        grad_u = jnp.dot(err[...], vb[...], preferred_element_type=jnp.float32)
        users = inb[slot, c]
        outb[slot, c] = users - step_size * (grad_u + LAMBDA * users)

        for n in range(items // TILE):
            cols = pl.ds(n * TILE, TILE)
            gv[cols, :] += lax.dot_general(err[:, cols], users_bf, (((0,), (0,)), ((), ())), preferred_element_type=jnp.float32)

        @pl.when(t < epochs_t - 2)
        def _():
            pl.semaphore_signal(credit, inc=1, device_id=(rep, right), device_id_type=MESH)

        @pl.when((t > 0) & (t < epochs_t - 1))
        def _():
            pl.semaphore_wait(credit, 1)

        @pl.when(t < epochs_t - 1)
        def _():
            send(t, c).start()

        @pl.when(t == epochs_t - 1)
        def _():
            send_home(t, c).start()

    def sub_epoch(first, t, carry):
        step_size = base_eta * lr_ref[t, 0]

        def body(c, inner):
            chunk_step(t, c, step_size, first)
            return inner

        lax.fori_loop(0, chunks, body, 0)
        for n in range(items // TILE):
            cols = pl.ds(n * TILE, TILE)
            old = v[cols, :]
            new = old - step_size * (gv[cols, :] + LAMBDA * old)
            v[cols, :] = new
            vb[cols, :] = new.astype(jnp.bfloat16)
            gv[cols, :] = jnp.zeros((TILE, v.shape[1]), jnp.float32)
        return carry

    lax.fori_loop(0, group, functools.partial(sub_epoch, True), 0)
    lax.fori_loop(group, epochs_t, functools.partial(sub_epoch, False), 0)

    v_store = pltpu.make_async_copy(v, vo_hbm, load_sem)
    v_store.start()
    v_store.wait()
    for c in range(chunks):
        send(epochs_t - 2, c).wait_send()
        send_home(epochs_t - 1, c).wait_send()
        send_home(epochs_t - 1, c).wait_recv()


def solution(mesh):
    group = mesh.shape["blk"]

    def local_run(rate_loc, mask_loc, user_loc, item_loc, lr_scale):
        block_rows, rank = user_loc.shape
        items = item_loc.shape[0]
        epochs_t = lr_scale.shape[0]
        chunks = block_rows // CHUNK
        base_eta = math.sqrt(rank) / (4.0 * (items + 2 * rank))
        hbm = pl.BlockSpec(memory_space=pl.ANY)
        return pl.pallas_call(
            functools.partial(run_kernel, group, epochs_t, base_eta),
            out_shape=(jax.ShapeDtypeStruct(user_loc.shape, jnp.float32), jax.ShapeDtypeStruct(item_loc.shape, jnp.float32)),
            in_specs=[pl.BlockSpec(memory_space=pltpu.SMEM), hbm, hbm, hbm, hbm],
            out_specs=(hbm, hbm),
            scratch_shapes=[
                pltpu.VMEM((group * chunks, CHUNK, items), jnp.float32),
                pltpu.VMEM((STAGES, CHUNK, items), jnp.int32),
                pltpu.VMEM((items, rank), jnp.float32),
                pltpu.VMEM((items, rank), jnp.bfloat16),
                pltpu.VMEM((items, rank), jnp.float32),
                pltpu.VMEM((CHUNK, items), jnp.bfloat16),
                pltpu.VMEM((2, chunks, CHUNK, rank), jnp.float32),
                pltpu.VMEM((2, chunks, CHUNK, rank), jnp.float32),
                pltpu.SemaphoreType.DMA,
                pltpu.SemaphoreType.DMA((STAGES,)),
                pltpu.SemaphoreType.DMA((STAGES,)),
                pltpu.SemaphoreType.DMA((2, chunks)),
                pltpu.SemaphoreType.DMA((2, chunks)),
                pltpu.SemaphoreType.DMA((chunks,)),
                pltpu.SemaphoreType.REGULAR,
            ],
            compiler_params=pltpu.CompilerParams(collective_id=0, has_side_effects=True, vmem_limit_bytes=67_043_328),
        )(lr_scale, rate_loc, mask_loc, user_loc, item_loc)

    spec_cols = P(None, ("rep", "blk"))
    spec_rows = P(("rep", "blk"), None)
    return jax.shard_map(local_run, mesh=mesh, in_specs=(spec_cols, spec_cols, spec_rows, spec_rows, P(None, None)),
                         out_specs=(spec_rows, spec_rows), check_vma=False)
```

time: 1690 us -> 735 us (0.43)
  matrix products: 954 us -> 0 us
  Pallas kernels: 0 us -> 729 us
  waiting for transfers between devices: 597 us -> 0 us
  local copies, waits for them, and re-layouts: 82.2 us -> 5.09 us
  other arithmetic: 42.6 us -> 0 us
    dot_general x192 -> x0, matrix products: 954 us -> none  [the longest x64 452 us: one_step(): jnp.einsum('ar,br->ab', users_bf, items_bf, preferred_element_type=jnp.fl...]
    pallas_call x0 -> x1, Pallas kernels: none -> 729 us  [local_run(): pl.pallas_call(functools.partial(run_kernel, group, epochs_t, base_eta),...]
    ppermute x64 -> x0, waiting for transfers between devices: 597 us -> none  [sub_epoch(): users_cur = lax.ppermute(users_cur, 'blk', send_perm)]
    while x192 -> x0, local copies, waits for them, and re-layouts: 78.7 us -> none
    mul x64 -> x0, other arithmetic: 42.6 us -> none  [one_step(): step_size = base_eta * lr_row[step_idx]]
  transfers between devices with their start and end apart: 64 -> 0, of which waited for: 64 -> 0; matrix products, arithmetic and copies ran while one was open for 19% -> 0% of each run, Pallas kernels for 0% -> 0%
where the time goes in v1:
time: 735 us
  Pallas kernels  729 us (99%)
    pallas_call x1, Pallas kernels, local_run(): pl.pallas_call(functools.partial(run_kernel, group, epochs_t, base_eta),...  729 us

profile of v1, /device:TPU:1, one launch (start us, length us, event | category | flops | bytes accessed | tf_op | source)
XLA Modules:
  0.0 734.6 jit_solution(3110044639096233385)
XLA Ops:
  0.6 1.4 copy.7.lr_ref
  2.0 728.9 %shard_map.68 = (f32[1024,256]{1,0:T(8,128)}, f32[2048,256]{1,0:T(8,128)}) custom-call(f32[64,1]{1,0:T(8,128)} %copy.7.lr_ref, f32[4096,2048]{1,0:T(8,128)} %r_hbm.1, s32[4096,2048]{1,0:T(8,128)} %m_hbm.1, f32[1024,256]{1,0:T(8,128)} %u_hbm.1, f32[2048,256]{1,0:T(8,128)} %v_hbm.1), custom_call_target="tpu_custom_call" | custom-call | tf_op jit(solution)/shard_map/pallas_call | solution.py:172
  730.9 0.0 copy-start
  730.9 2.4 copy.10
  733.3 0.0 copy-done
  733.3 1.3 copy.11
Async XLA Ops:
  730.9 2.4 copy-start

commit v2 on v1

--- a/solution.py
+++ b/solution.py
@@ -10,13 +10,13 @@
 
 LAMBDA = 0.05
 MESH = pl.DeviceIdType.MESH
-CHUNK = 256
+CHUNK = 128
 TILE = 512
 STAGES = 3
 
 
-def run_kernel(group, epochs_t, base_eta, lr_ref, r_hbm, m_hbm, u_hbm, v_hbm, uo_hbm, vo_hbm,
-               rate, mask, v, vb, gv, err, inb, outb, load_sem, r_sem, m_sem, send_sem, recv_sem, home_sem, credit):
+def run_kernel(group, epochs_t, base_eta, lr_hbm, r_hbm, m_hbm, u_hbm, v_hbm, uo_hbm, vo_hbm,
+               lr, rate, mask, v, vb, gv, err, inb, outb, load_sem, r_sem, m_sem, send_sem, recv_sem, home_sem, lr_sem, credit):
     rep, me = lax.axis_index("rep"), lax.axis_index("blk")
     left, right = lax.rem(me + group - 1, group), lax.rem(me + 1, group)
     chunks = inb.shape[1]
@@ -50,24 +50,33 @@
     def user_load(c):
         return pltpu.make_async_copy(u_hbm.at[pl.ds(c * CHUNK, CHUNK)], inb.at[0, c], recv_sem.at[0, c])
 
-    v_load = pltpu.make_async_copy(v_hbm, v, load_sem)
-    v_load.start()
+    def v_load(n):
+        cols = pl.ds(n * TILE, TILE)
+        return pltpu.make_async_copy(v_hbm.at[cols], v.at[cols], load_sem.at[n])
+
+    tiles = items // TILE
+    for n in range(tiles):
+        v_load(n).start()
     user_load(0).start()
     rate_load(0).start()
     mask_load(0).start()
+    lr_load = pltpu.make_async_copy(lr_hbm, lr, lr_sem)
+    lr_load.start()
     for c in range(1, chunks):
         user_load(c).start()
-    rate_load(1).start()
-    mask_load(1).start()
 
     barrier = pltpu.get_barrier_semaphore()
     for neighbour in (left, right):
         pl.semaphore_signal(barrier, inc=1, device_id=(rep, neighbour), device_id_type=MESH)
+    gv[...] = jnp.zeros_like(gv)
+    for n in range(tiles):
+        cols = pl.ds(n * TILE, TILE)
+        v_load(n).wait()
+        vb[cols, :] = v[cols, :].astype(jnp.bfloat16)
+    lr_load.wait()
     pl.semaphore_wait(barrier, 2)
-
-    gv[...] = jnp.zeros_like(gv)
-    v_load.wait()
-    vb[...] = v[...].astype(jnp.bfloat16)
+    rate_load(1).start()
+    mask_load(1).start()
 
     def chunk_step(t, c, step_size, first):
         slot = lax.rem(t, 2)
@@ -131,7 +140,7 @@
             send_home(t, c).start()
 
     def sub_epoch(first, t, carry):
-        step_size = base_eta * lr_ref[t, 0]
+        step_size = base_eta * lr[t]
 
         def body(c, inner):
             chunk_step(t, c, step_size, first)
@@ -150,49 +159,74 @@
     lax.fori_loop(0, group, functools.partial(sub_epoch, True), 0)
     lax.fori_loop(group, epochs_t, functools.partial(sub_epoch, False), 0)
 
-    v_store = pltpu.make_async_copy(v, vo_hbm, load_sem)
-    v_store.start()
-    v_store.wait()
+    vo_hbm[...] = v[...]
     for c in range(chunks):
         send(epochs_t - 2, c).wait_send()
         send_home(epochs_t - 1, c).wait_send()
         send_home(epochs_t - 1, c).wait_recv()
 
 
+PARTS = 4
+
+
+def write_out(u_vmem, v_vmem, uo_hbm, vo_hbm, sem):
+    copies = []
+    for k, (src, dst) in enumerate(((v_vmem, vo_hbm), (u_vmem, uo_hbm))):
+        rows = src.shape[0] // PARTS
+        for p in range(PARTS):
+            part = pl.ds(p * rows, rows)
+            copies.append(pltpu.make_async_copy(src.at[part], dst.at[part], sem.at[k, p]))
+    for copy in copies:
+        copy.start()
+    for copy in copies:
+        copy.wait()
+
+
 def solution(mesh):
     group = mesh.shape["blk"]
 
     def local_run(rate_loc, mask_loc, user_loc, item_loc, lr_scale):
         block_rows, rank = user_loc.shape
-        items = item_loc.shape[0]
+        cols = item_loc.shape[0]
         epochs_t = lr_scale.shape[0]
         chunks = block_rows // CHUNK
-        base_eta = math.sqrt(rank) / (4.0 * (items + 2 * rank))
+        base_eta = math.sqrt(rank) / (4.0 * (cols + 2 * rank))
+        vmem = pl.BlockSpec(memory_space=pltpu.VMEM)
         hbm = pl.BlockSpec(memory_space=pl.ANY)
-        return pl.pallas_call(
+        users, items = pl.pallas_call(
             functools.partial(run_kernel, group, epochs_t, base_eta),
-            out_shape=(jax.ShapeDtypeStruct(user_loc.shape, jnp.float32), jax.ShapeDtypeStruct(item_loc.shape, jnp.float32)),
-            in_specs=[pl.BlockSpec(memory_space=pltpu.SMEM), hbm, hbm, hbm, hbm],
-            out_specs=(hbm, hbm),
+            out_shape=(pltpu.VMEM(user_loc.shape, jnp.float32), pltpu.VMEM(item_loc.shape, jnp.float32)),
+            in_specs=[hbm, hbm, hbm, hbm, hbm],
+            out_specs=(vmem, vmem),
             scratch_shapes=[
-                pltpu.VMEM((group * chunks, CHUNK, items), jnp.float32),
-                pltpu.VMEM((STAGES, CHUNK, items), jnp.int32),
-                pltpu.VMEM((items, rank), jnp.float32),
-                pltpu.VMEM((items, rank), jnp.bfloat16),
-                pltpu.VMEM((items, rank), jnp.float32),
-                pltpu.VMEM((CHUNK, items), jnp.bfloat16),
+                pltpu.SMEM((epochs_t,), jnp.float32),
+                pltpu.VMEM((group * chunks, CHUNK, cols), jnp.float32),
+                pltpu.VMEM((STAGES, CHUNK, cols), jnp.int32),
+                pltpu.VMEM((cols, rank), jnp.float32),
+                pltpu.VMEM((cols, rank), jnp.bfloat16),
+                pltpu.VMEM((cols, rank), jnp.float32),
+                pltpu.VMEM((CHUNK, cols), jnp.bfloat16),
                 pltpu.VMEM((2, chunks, CHUNK, rank), jnp.float32),
                 pltpu.VMEM((2, chunks, CHUNK, rank), jnp.float32),
-                pltpu.SemaphoreType.DMA,
+                pltpu.SemaphoreType.DMA((cols // TILE,)),
                 pltpu.SemaphoreType.DMA((STAGES,)),
                 pltpu.SemaphoreType.DMA((STAGES,)),
                 pltpu.SemaphoreType.DMA((2, chunks)),
                 pltpu.SemaphoreType.DMA((2, chunks)),
                 pltpu.SemaphoreType.DMA((chunks,)),
+                pltpu.SemaphoreType.DMA,
                 pltpu.SemaphoreType.REGULAR,
             ],
-            compiler_params=pltpu.CompilerParams(collective_id=0, has_side_effects=True, vmem_limit_bytes=67_043_328),
-        )(lr_scale, rate_loc, mask_loc, user_loc, item_loc)
+            compiler_params=pltpu.CompilerParams(collective_id=0, has_side_effects=True, vmem_limit_bytes=56*1024*1024),
+        )(lr_scale.reshape(epochs_t), rate_loc, mask_loc, user_loc, item_loc)
+        return pl.pallas_call(
+            write_out,
+            out_shape=(jax.ShapeDtypeStruct(user_loc.shape, jnp.float32), jax.ShapeDtypeStruct(item_loc.shape, jnp.float32)),
+            in_specs=[vmem, vmem],
+            out_specs=(hbm, hbm),
+            scratch_shapes=[pltpu.SemaphoreType.DMA((2, PARTS))],
+            compiler_params=pltpu.CompilerParams(vmem_limit_bytes=1024 * 1024),
+        )(users, items)
 
     spec_cols = P(None, ("rep", "blk"))
     spec_rows = P(("rep", "blk"), None)

time: 735 us -> 730 us (level)
  no operation moved by 1% of the time
where the time goes in v2:
time: 730 us; the launch traced here: 729 us
  Pallas kernels  729 us (100%)
    pallas_call x1, Pallas kernels, local_run(): pl.pallas_call(functools.partial(run_kernel, group, epochs_t, base_eta),...  727 us

profile of v2, /device:TPU:1, one launch (start us, length us, event | category | flops | bytes accessed | tf_op | source)
XLA Modules:
  0.0 729.4 jit_solution(16978549945106787917)
XLA Ops:
  0.6 727.1 %shard_map.68 = (f32[1024,256]{1,0:T(8,128)S(1)}, f32[2048,256]{1,0:T(8,128)S(1)}) custom-call(f32[64]{0:T(128)} %bitcast.1, f32[4096,2048]{1,0:T(8,128)} %r_hbm.1, s32[4096,2048]{1,0:T(8,128)} %m_hbm.1, f32[1024,256]{1,0:T(8,128)} %u_hbm.1, f32[2048,256]{1,0:T(8,128)} %v_hbm.1), custom_call_target="tpu_custom_call" | custom-call | tf_op jit(solution)/shard_map/pallas_call | solution.py:196
  727.7 1.7 shard_map.69

commit v3 on v2

--- a/solution.py
+++ b/solution.py
@@ -62,8 +62,6 @@
     mask_load(0).start()
     lr_load = pltpu.make_async_copy(lr_hbm, lr, lr_sem)
     lr_load.start()
-    for c in range(1, chunks):
-        user_load(c).start()
 
     barrier = pltpu.get_barrier_semaphore()
     for neighbour in (left, right):
@@ -77,6 +75,8 @@
     pl.semaphore_wait(barrier, 2)
     rate_load(1).start()
     mask_load(1).start()
+    for c in range(1, chunks):
+        user_load(c).start()
 
     def chunk_step(t, c, step_size, first):
         slot = lax.rem(t, 2)
@@ -166,7 +166,7 @@
         send_home(epochs_t - 1, c).wait_recv()
 
 
-PARTS = 4
+PARTS = 2
 
 
 def write_out(u_vmem, v_vmem, uo_hbm, vo_hbm, sem):

time: 730 us -> 729 us (level)
  no operation moved by 1% of the time
where the time goes in v3:
time: 729 us
  Pallas kernels  728 us (100%)
    pallas_call x1, Pallas kernels, local_run(): pl.pallas_call(functools.partial(run_kernel, group, epochs_t, base_eta),...  727 us

profile of v3, /device:TPU:1, one launch (start us, length us, event | category | flops | bytes accessed | tf_op | source)
XLA Modules:
  0.0 729.1 jit_solution(8419758909294788727)
XLA Ops:
  0.6 726.7 %shard_map.68 = (f32[1024,256]{1,0:T(8,128)S(1)}, f32[2048,256]{1,0:T(8,128)S(1)}) custom-call(f32[64]{0:T(128)} %bitcast.1, f32[4096,2048]{1,0:T(8,128)} %r_hbm.1, s32[4096,2048]{1,0:T(8,128)} %m_hbm.1, f32[1024,256]{1,0:T(8,128)} %u_hbm.1, f32[2048,256]{1,0:T(8,128)} %v_hbm.1), custom_call_target="tpu_custom_call" | custom-call | tf_op jit(solution)/shard_map/pallas_call | solution.py:196
  727.4 1.7 shard_map.69

commit v4 on v3

--- a/solution.py
+++ b/solution.py
@@ -11,7 +11,8 @@
 LAMBDA = 0.05
 MESH = pl.DeviceIdType.MESH
 CHUNK = 128
-TILE = 512
+TILE = 1024
+STRIP = 128
 STAGES = 3
 
 
@@ -60,21 +61,30 @@
     user_load(0).start()
     rate_load(0).start()
     mask_load(0).start()
+    rate_load(1).start()
+    mask_load(1).start()
     lr_load = pltpu.make_async_copy(lr_hbm, lr, lr_sem)
     lr_load.start()
 
     barrier = pltpu.get_barrier_semaphore()
     for neighbour in (left, right):
         pl.semaphore_signal(barrier, inc=1, device_id=(rep, neighbour), device_id_type=MESH)
-    gv[...] = jnp.zeros_like(gv)
+
+    def clear(n, carry):
+        gv[pl.ds(pl.multiple_of(n * STRIP, STRIP), STRIP), :] = jnp.zeros((STRIP, gv.shape[1]), jnp.float32)
+        return carry
+
+    def convert(n, carry):
+        cols = pl.ds(pl.multiple_of(n * STRIP, STRIP), STRIP)
+        vb[cols, :] = v[cols, :].astype(jnp.bfloat16)
+        return carry
+
+    lax.fori_loop(0, items // STRIP, clear, 0)
     for n in range(tiles):
-        cols = pl.ds(n * TILE, TILE)
         v_load(n).wait()
-        vb[cols, :] = v[cols, :].astype(jnp.bfloat16)
+        lax.fori_loop(n * TILE // STRIP, (n + 1) * TILE // STRIP, convert, 0)
     lr_load.wait()
     pl.semaphore_wait(barrier, 2)
-    rate_load(1).start()
-    mask_load(1).start()
     for c in range(1, chunks):
         user_load(c).start()
 
@@ -147,13 +157,17 @@
             return inner
 
         lax.fori_loop(0, chunks, body, 0)
-        for n in range(items // TILE):
-            cols = pl.ds(n * TILE, TILE)
+
+        def update(n, inner):
+            cols = pl.ds(pl.multiple_of(n * STRIP, STRIP), STRIP)
             old = v[cols, :]
             new = old - step_size * (gv[cols, :] + LAMBDA * old)
             v[cols, :] = new
             vb[cols, :] = new.astype(jnp.bfloat16)
-            gv[cols, :] = jnp.zeros((TILE, v.shape[1]), jnp.float32)
+            gv[cols, :] = jnp.zeros((STRIP, v.shape[1]), jnp.float32)
+            return inner
+
+        lax.fori_loop(0, items // STRIP, update, 0)
         return carry
 
     lax.fori_loop(0, group, functools.partial(sub_epoch, True), 0)
@@ -166,7 +180,7 @@
         send_home(epochs_t - 1, c).wait_recv()
 
 
-PARTS = 2
+PARTS = 1
 
 
 def write_out(u_vmem, v_vmem, uo_hbm, vo_hbm, sem):

time: 729 us -> 729 us (level)
  no operation moved by 1% of the time
where the time goes in v4:
time: 729 us
  Pallas kernels  728 us (100%)
    pallas_call x1, Pallas kernels, local_run(): pl.pallas_call(functools.partial(run_kernel, group, epochs_t, base_eta),...  727 us

profile of v4, /device:TPU:1, one launch (start us, length us, event | category | flops | bytes accessed | tf_op | source)
XLA Modules:
  0.0 729.0 jit_solution(12481368087518499312)
XLA Ops:
  0.6 726.7 %shard_map.68 = (f32[1024,256]{1,0:T(8,128)S(1)}, f32[2048,256]{1,0:T(8,128)S(1)}) custom-call(f32[64]{0:T(128)} %bitcast.1, f32[4096,2048]{1,0:T(8,128)} %r_hbm.1, s32[4096,2048]{1,0:T(8,128)} %m_hbm.1, f32[1024,256]{1,0:T(8,128)} %u_hbm.1, f32[2048,256]{1,0:T(8,128)} %v_hbm.1), custom_call_target="tpu_custom_call" | custom-call | tf_op jit(solution)/shard_map/pallas_call | solution.py:210
  727.3 1.7 shard_map.69

commit v5 on v4

--- a/solution.py
+++ b/solution.py
@@ -83,10 +83,10 @@
     for n in range(tiles):
         v_load(n).wait()
         lax.fori_loop(n * TILE // STRIP, (n + 1) * TILE // STRIP, convert, 0)
+    for c in range(1, chunks):
+        user_load(c).start()
     lr_load.wait()
     pl.semaphore_wait(barrier, 2)
-    for c in range(1, chunks):
-        user_load(c).start()
 
     def chunk_step(t, c, step_size, first):
         slot = lax.rem(t, 2)

time: 729 us -> 729 us (level)
  no operation moved by 1% of the time
where the time goes in v5:
time: 729 us
  Pallas kernels  728 us (100%)
    pallas_call x1, Pallas kernels, local_run(): pl.pallas_call(functools.partial(run_kernel, group, epochs_t, base_eta),...  727 us

profile of v5, /device:TPU:1, one launch (start us, length us, event | category | flops | bytes accessed | tf_op | source)
XLA Modules:
  0.0 729.0 jit_solution(2708613661209556471)
XLA Ops:
  0.6 726.7 %shard_map.68 = (f32[1024,256]{1,0:T(8,128)S(1)}, f32[2048,256]{1,0:T(8,128)S(1)}) custom-call(f32[64]{0:T(128)} %bitcast.1, f32[4096,2048]{1,0:T(8,128)} %r_hbm.1, s32[4096,2048]{1,0:T(8,128)} %m_hbm.1, f32[1024,256]{1,0:T(8,128)} %u_hbm.1, f32[2048,256]{1,0:T(8,128)} %v_hbm.1), custom_call_target="tpu_custom_call" | custom-call | tf_op jit(solution)/shard_map/pallas_call | solution.py:210
  727.3 1.7 shard_map.69
